TPU v7x, 32 devices: a whole 2x2x4 slice. The times are simulated.
32 devices in a mesh: dp: 8 (over z, x), tensor: 4 (over y, core).
Axes of the slice: x: 2, y: 2, z: 4, core: 2. Of those that a mesh axis runs over, the one named last changes fastest.
Arguments:
- tokens: bfloat16 [64, 258, 768], P('dp'), may hold values from -6 to 6
- metadata: int32 [64], P('dp'), may hold values 0 or 1
- cotangent: bfloat16 [64, 258, 768], P('dp'), may hold values from -6 to 6
- w_query: bfloat16 [768, 768], P(None, 'tensor'), may hold values from -0.21875 to 0.21875
- w_key: bfloat16 [768, 768], P(None, 'tensor'), may hold values from -0.21875 to 0.21875
- w_value: bfloat16 [768, 768], P(None, 'tensor'), may hold values from -0.21875 to 0.21875
- w_out: bfloat16 [768, 768], P('tensor'), may hold values from -1.75 to 1.75
- b_query: float32 [768], P('tensor'), may hold values from -1.5 to 1.5
- b_value: float32 [768], P('tensor'), may hold values from -1.5 to 1.5
- b_out: float32 [768], replicated, may hold values from -1.5 to 1.5
- w_up: bfloat16 [768, 3072], P(None, 'tensor'), may hold values from -0.21875 to 0.21875
- b_up: float32 [3072], P('tensor'), may hold values from -1.5 to 1.5
- w_down: bfloat16 [3072, 768], P('tensor'), may hold values from -0.21875 to 0.21875
- b_down: float32 [768], replicated, may hold values from -1.5 to 1.5
- gain_one: float32 [768], replicated, may hold values from 0.25 to 1.75
- shift_one: float32 [768], replicated, may hold values from -1.5 to 1.5
- gain_two: float32 [768], replicated, may hold values from 0.25 to 1.75
- shift_two: float32 [768], replicated, may hold values from -1.5 to 1.5
Outputs:
- layer_out: bfloat16 [64, 258, 768], P('dp')
- grad_tokens: float32 [64, 258, 768], P('dp')
- grad_w_query: float32 [768, 768], P(None, 'tensor')
- grad_w_key: float32 [768, 768], P(None, 'tensor')
- grad_w_value: float32 [768, 768], P(None, 'tensor')
- grad_w_out: float32 [768, 768], P('tensor')
- grad_b_query: float32 [768], P('tensor')
- grad_b_value: float32 [768], P('tensor')
- grad_b_out: float32 [768], replicated
- grad_w_up: float32 [768, 3072], P(None, 'tensor')
- grad_b_up: float32 [3072], P('tensor')
- grad_w_down: float32 [3072, 768], P('tensor')
- grad_b_down: float32 [768], replicated
- grad_gain_one: float32 [768], replicated
- grad_shift_one: float32 [768], replicated
- grad_gain_two: float32 [768], replicated
- grad_shift_two: float32 [768], replicated
All inputs are finite; a program needn't handle non-finite values. No bound on the sum of `metadata` on one device may be relied on, other than what follows from the above.
Results may differ from a plain program's by a relative error of at most 0.012.
Values sent between devices are 32-bit elements; how exact they have to be, the bound alone decides.
A program may use at most 192 MiB of HBM per device.

v0:
```python
import math
import jax
import jax.numpy as jnp
from jax import lax
from jax.sharding import PartitionSpec as P

HEAD_DIM = 64
NORM_EPSILON = 1e-05


def layer_norm(source_tokens, gain, shift):
    average = jnp.mean(source_tokens, -1, keepdims=True)
    mean_removed = source_tokens - average
    variance = jnp.mean(mean_removed * mean_removed, -1, keepdims=True)
    return mean_removed * lax.rsqrt(variance + NORM_EPSILON) * gain + shift


def gelu_exact(source_tokens):
    return jax.nn.gelu(source_tokens, approximate=False)


def multiply(left_mat, right_mat):
    return jnp.dot(left_mat, right_mat, preferred_element_type=jnp.float32)


def contract_rows(left_mat, right_mat):
    return lax.dot_general(
        left_mat, right_mat, (((0,), (0,)), ((), ())), preferred_element_type=jnp.float32
    )


def contract_cols(left_mat, right_mat):
    return lax.dot_general(
        left_mat, right_mat, (((1,), (1,)), ((), ())), preferred_element_type=jnp.float32
    )


def column_sums(matrix):
    return jnp.sum(matrix.astype(jnp.float32), 0)


def shards(
    tokens,
    metadata,
    cotangent,
    w_query,
    w_key,
    w_value,
    w_out,
    b_query,
    b_value,
    b_out,
    w_up,
    b_up,
    w_down,
    b_down,
    gain_one,
    shift_one,
    gain_two,
    shift_two,
):
    samples, length, model_width = tokens.shape
    row_count = samples * length
    local_width = w_query.shape[1]
    local_heads = local_width // HEAD_DIM
    score_scale = 1.0 / math.sqrt(HEAD_DIM)
    position = lax.broadcasted_iota(jnp.int32, (samples, length), 1)
    keep_mask = jnp.where(
        position == 1, metadata[:, None].astype(jnp.float32), jnp.float32(1.0)
    ).reshape(row_count, 1)
    inputs = tokens.reshape(row_count, model_width).astype(jnp.float32) * keep_mask

    def split_heads(matrix):
        return matrix.reshape(samples, length, local_heads, HEAD_DIM)

    normed, first_norm_backward = jax.vjp(layer_norm, inputs, gain_one, shift_one)
    normed_low = normed.astype(jnp.bfloat16)
    queries = (multiply(normed_low, w_query) + b_query).astype(jnp.bfloat16)
    key_rows = multiply(normed_low, w_key).astype(jnp.bfloat16)
    values = (multiply(normed_low, w_value) + b_value).astype(jnp.bfloat16)
    head_queries = split_heads(queries)
    head_keys = split_heads(key_rows)
    head_values = split_heads(values)
    scores = (
        jnp.einsum("sqhc,skhc->shqk", head_queries, head_keys, preferred_element_type=jnp.float32)
        * score_scale
    )
    row_max = jnp.max(scores, -1, keepdims=True)
    row_total = jnp.sum(jnp.exp(scores - row_max), -1, keepdims=True)
    logsum = row_max + jnp.log(row_total)
    probs_low = jnp.exp(scores - logsum).astype(jnp.bfloat16)
    mixture = jnp.einsum(
        "shqk,skhc->sqhc", probs_low, head_values, preferred_element_type=jnp.float32
    )
    mixture = mixture.reshape(row_count, local_width).astype(jnp.bfloat16)
    branch = lax.psum(multiply(mixture, w_out), "tensor") + b_out
    middle = inputs + branch
    normed_two, norm_two_back = jax.vjp(layer_norm, middle, gain_two, shift_two)
    normed_two_low = normed_two.astype(jnp.bfloat16)
    hidden = multiply(normed_two_low, w_up) + b_up
    active, gelu_back = jax.vjp(gelu_exact, hidden)
    active_reduced = active.astype(jnp.bfloat16)
    branch_two = lax.psum(multiply(active_reduced, w_down), "tensor") + b_down
    layer_out = (middle + branch_two).astype(jnp.bfloat16).reshape(samples, length, model_width)
    grad_out = cotangent.reshape(row_count, model_width).astype(jnp.float32)
    grad_out_low = grad_out.astype(jnp.bfloat16)
    grad_b_down = column_sums(grad_out_low)
    grad_w_down = contract_rows(active_reduced, grad_out_low)
    grad_active = contract_cols(grad_out_low, w_down)
    grad_hidden = gelu_back(grad_active)[0].astype(jnp.bfloat16)
    grad_b_up = column_sums(grad_hidden)
    grad_w_up = contract_rows(normed_two_low, grad_hidden)
    grad_normed_two = lax.psum(contract_cols(grad_hidden, w_up), "tensor")
    grad_mid_part, grad_gain_two, grad_shift_two = norm_two_back(grad_normed_two)
    grad_middle = grad_out + grad_mid_part
    mlp_group = (grad_w_up, grad_b_up, grad_w_down, grad_b_down, grad_gain_two, grad_shift_two)
    grad_mid_low = grad_middle.astype(jnp.bfloat16)
    grad_b_out = column_sums(grad_mid_low)
    grad_w_out = contract_rows(mixture, grad_mid_low)
    grad_mixture = split_heads(contract_cols(grad_mid_low, w_out).astype(jnp.bfloat16))
    scores_again = (
        jnp.einsum("sqhc,skhc->shqk", head_queries, head_keys, preferred_element_type=jnp.float32)
        * score_scale
    )
    attn_probs = jnp.exp(scores_again - logsum)
    probs_again = attn_probs.astype(jnp.bfloat16)
    grad_values = jnp.einsum(
        "shqk,sqhc->skhc", probs_again, grad_mixture, preferred_element_type=jnp.float32
    )
    grad_values = grad_values.reshape(row_count, local_width).astype(jnp.bfloat16)
    grad_probs = jnp.einsum(
        "sqhc,skhc->shqk", grad_mixture, head_values, preferred_element_type=jnp.float32
    )
    grad_scores = attn_probs * (grad_probs - jnp.sum(attn_probs * grad_probs, -1, keepdims=True))
    grad_scores = grad_scores.astype(jnp.bfloat16)
    grad_queries = (
        jnp.einsum("shqk,skhc->sqhc", grad_scores, head_keys, preferred_element_type=jnp.float32)
        * score_scale
    )
    grad_queries = grad_queries.reshape(row_count, local_width).astype(jnp.bfloat16)
    grad_keys = (
        jnp.einsum("shqk,sqhc->skhc", grad_scores, head_queries, preferred_element_type=jnp.float32)
        * score_scale
    )
    grad_keys = grad_keys.reshape(row_count, local_width).astype(jnp.bfloat16)
    grad_w_query = contract_rows(normed_low, grad_queries)
    grad_w_key = contract_rows(normed_low, grad_keys)
    grad_w_value = contract_rows(normed_low, grad_values)
    grad_b_query = column_sums(grad_queries)
    grad_b_value = column_sums(grad_values)
    grad_normalized_piece = (
        contract_cols(grad_queries, w_query)
        + contract_cols(grad_keys, w_key)
        + contract_cols(grad_values, w_value)
    )
    grad_normed = lax.psum(grad_normalized_piece, "tensor")
    grad_in_part, grad_gain_one, grad_shift_one = first_norm_backward(grad_normed)
    grad_tokens = ((grad_middle + grad_in_part) * keep_mask).reshape(samples, length, model_width)
    attn_group = (
        grad_w_query,
        grad_w_key,
        grad_w_value,
        grad_w_out,
        grad_b_query,
        grad_b_value,
        grad_b_out,
        grad_gain_one,
        grad_shift_one,
    )
    summed = lax.psum(mlp_group + attn_group, "dp")
    mlp_group = summed[:6]
    attn_group = summed[6:]
    return (
        layer_out,
        grad_tokens,
        attn_group[0],
        attn_group[1],
        attn_group[2],
        attn_group[3],
        attn_group[4],
        attn_group[5],
        attn_group[6],
        mlp_group[0],
        mlp_group[1],
        mlp_group[2],
        mlp_group[3],
        attn_group[7],
        attn_group[8],
        mlp_group[4],
        mlp_group[5],
    )


def solution(mesh):
    return jax.shard_map(
        shards,
        mesh=mesh,
        in_specs=(
            P("dp", None, None),
            P("dp"),
            P("dp", None, None),
            P(None, "tensor"),
            P(None, "tensor"),
            P(None, "tensor"),
            P("tensor", None),
            P("tensor"),
            P("tensor"),
            P(),
            P(None, "tensor"),
            P("tensor"),
            P("tensor", None),
            P(),
            P(),
            P(),
            P(),
            P(),
        ),
        out_specs=(
            P("dp", None, None),
            P("dp", None, None),
            P(None, "tensor"),
            P(None, "tensor"),
            P(None, "tensor"),
            P("tensor", None),
            P("tensor"),
            P("tensor"),
            P(),
            P(None, "tensor"),
            P("tensor"),
            P("tensor", None),
            P(),
            P(),
            P(),
            P(),
            P(),
        ),
        check_vma=False,
    )
```

profile of v0, /device:TPU:0, one launch (start us, length us, event | category | flops | bytes accessed | tf_op | source)
XLA Modules:
  0.0 897.8 jit_solution(9342128070286131994)
XLA Ops:
  8.3 2.7 multiply_reduce_fusion.8
  11.4 5.4 copy.99
  19.3 5.0 reshape.276
  24.4 3.7 add_convert_fusion.4
  32.4 3.6 fusion.8
  36.0 2.4 reshape.269
  38.4 4.0 fusion.9
  42.4 3.0 reshape.270
  45.4 1.9 multiply_reduce_fusion.1
  47.4 1.8 exponential_reduce_fusion
  49.5 2.1 fusion.10
  51.6 1.7 copy.108
  53.3 2.1 convert_element_type.138
  55.4 3.7 fusion.35
  59.2 4.2 copy.109
  63.5 3.7 reshape.273
  67.2 115.4 %all-reduce.8.cloned.1.call-done = f32[2064,768]{1,0:T(8,128)} async-done(((f32[2064,768]{1,0:T(8,128)}), f32[2064,768]{1,0:T(8,128)}) %all-reduce.8.cloned.1.call-update) | async-done | bytes 6340624 | tf_op jit(solution)/shard_map/psum | solution.py:96
  182.6 5.8 fusion.34
  191.5 2.7 convolution_add_fusion
  194.6 18.7 %convert_reduce_fusion.1 = (f32[768]{0:T(1024)}, bf16[2064,768]{1,0:T(8,128)(2,1)S(1)}, f32[2064,768]{1,0:T(8,128)}) fusion(f32[2064,768]{1,0:T(8,128)S(1)} %convolution_add_fusion, bf16[2064,768]{1,0:T(8,128)(2,1)S(1)} %copy-done.8, bf16[768,768]{1,0:T(8,128)(2,1)S(1)} %copy-done), kind=kOutput, calls=%fused_computation.12 | convolution fusion | flops 2552093952 | bytes 20204544 | tf_op jit(solution)/shard_map/dot_general | solution.py:33
  213.3 1.7 copy-done.65
  215.0 4.6 fusion.37
  219.7 5.5 multiply_convert_fusion.1
  226.9 4.8 fusion.36
  231.6 108.8 %all-reduce.10.cloned.1.call-done = f32[2064,768]{1,0:T(8,128)} async-done(((f32[2064,768]{1,0:T(8,128)}), f32[2064,768]{1,0:T(8,128)}) %all-reduce.10.cloned.1.call-update) | async-done | bytes 6340624 | tf_op jit(solution)/shard_map/psum | solution.py:113
  340.5 6.5 multiply_reduce_fusion.2
  347.0 6.8 fusion.33
  353.8 2.5 convert_reduce_fusion.2
  356.5 1.7 copy-done.16
  360.8 6.8 convert_reduce_fusion.3
  367.6 7.8 multiply_reduce_fusion
  375.5 10.9 %multiply_convert_fusion = bf16[8,3,258,258]{2,3,1,0:T(8,128)(2,1)} fusion(f32[8,3,258,258]{2,3,1,0:T(8,128)} %get-tuple-element.124, f32[8,3,258,258]{2,3,1,0:T(8,128)} %copy-done.2, f32[8,3,258]{2,1,0:T(4,128)S(1)} %get-tuple-element.123, f32[8,3,258]{2,1,0:T(4,128)S(1)} %log_add_fusion), kind=kLoop, calls=%fused_computation | loop fusion | flops 7987680 | bytes 16024896 | tf_op jit(solution)/shard_map/convert_element_type | solution.py:135
  386.4 5.5 fusion.13
  393.3 1.7 copy.120
  395.0 2.1 convert_element_type.155
  397.1 3.3 copy.117
  400.4 2.1 convert_element_type.152
  404.2 2.1 convert_element_type.149
  408.4 3.7 add_add_fusion.2
  413.1 3.1 add_convert_fusion
  416.3 2.7 copy.122
  419.0 3.6 convert_element_type.157
  422.6 7.4 fusion.41
  430.0 4.4 fusion.42
  434.4 1.7 fusion.40
  436.1 1.7 fusion.45
  437.9 1.7 fusion.44
  439.6 1.7 fusion.43
  441.3 2.4 convert_reduce_fusion
  443.9 191.5 %all-reduce.14.cloned.1.call-done = (f32[2064,768]{1,0:T(8,128)}, f32[2064,768]{1,0:T(8,128)}) async-done(((f32[2064,768]{1,0:T(8,128)}, f32[2064,768]{1,0:T(8,128)}), (f32[2064,768]{1,0:T(8,128)}, f32[2064,768]{1,0:T(8,128)})) %all-reduce.14.cloned.1.call-update) | async-done | bytes 12681232 | tf_op jit(solution)/shard_map/psum | solution.py:103
  635.5 7.2 add_convert_fusion.2
  642.7 3.8 reshape.272
  646.5 5.0 copy.123
  651.5 7.1 multiply_reduce_fusion.3
  658.7 7.8 fusion.32
  666.5 7.5 add_multiply_fusion
  674.0 5.1 reshape.275
  679.1 7.7 copy.124
  686.8 39.8 %all-reduce = (f32[192]{0:T(256)}, f32[192]{0:T(256)}, f32[768]{0:T(1024)}, f32[768]{0:T(1024)}, f32[768]{0:T(1024)}, /*index=5*/f32[768]{0:T(1024)}, f32[768]{0:T(1024)}, f32[768]{0:T(1024)}, f32[768]{0:T(1024)}) all-reduce(f32[192]{0:T(256)S(1)} %reduce_sum.218, ...), channel_id=1, replica_groups=mesh['dp'=8,'tensor'=4] {'dp'}, use_global_device_ids=true, to_apply=%region_20.21 | all-reduce | flops 5760 | bytes 46080 | tf_op jit(solution)/shard_map/psum | solution.py:170
  726.6 153.7 %all-reduce.12.cloned.1.call-done = (f32[768,192]{0,1:T(8,128)}, f32[768,192]{0,1:T(8,128)}, f32[768,192]{0,1:T(8,128)}, f32[192,768]{1,0:T(8,128)}, f32[768,768]{1,0:T(8,128)}, /*index=5*/f32[768,768]{1,0:T(8,128)}) async-done(((f32[768,192]{0,1:T(8,128)}, f32[768,192]{0,1:T(8,128)}, f32[768,192]{0,1:T(8,128)}, f32[192,768]{1,0:T(8,128)}, f32[768,768]{1,0:T(8,128)}, /*index=5*/f32[768,768]{1,0:T(8,128)}), ...) | async-done | bytes 7077904 | tf_op jit(solution)/shard_map/psum | solution.py:170
  880.3 2.1 copy.167
  882.3 2.0 copy.168
  884.3 1.9 copy.169
  886.3 1.9 copy.170
  (179 shorter events, 25.7 us)
Async XLA Ops:
  7.2 187.1 %copy-start = (bf16[768,768]{1,0:T(8,128)(2,1)S(1)}, bf16[768,768]{1,0:T(8,128)(2,1)}, u32[]{:S(2)}) copy-start(bf16[768,768]{1,0:T(8,128)(2,1)} %param.30) | copy-start | bytes 3538948
  7.2 175.4 %all-reduce.8.cloned.1.call-start = ((), (), s32[]{:S(2)}) async-start(), calls=%async_computation | async-start | bytes 12681216 | tf_op jit(solution)/shard_map/psum | solution.py:96
  8.2 174.4 %copy-start.35 = (f32[2064]{0:T(1024)}, f32[2064]{0:T(1024)S(1)}, u32[]{:S(2)}) copy-start(f32[2064]{0:T(1024)S(1)} %select_n.13) | copy-start | bytes 24772
  8.3 8.5 copy-start.31
  11.3 13.1 %copy-start.43 = (f32[2064]{0:T(1024)}, f32[2064]{0:T(1024)S(1)}, u32[]{:S(2)}) copy-start(f32[2064]{0:T(1024)S(1)} %div.39) | copy-start | bytes 24772
  11.4 7.1 copy-start.33
  11.4 5.4 copy-start.7
  19.3 5.1 copy-start.47
  19.3 5.0 copy-start.45
  19.3 5.0 copy-start.49
  19.3 5.0 copy-start.55
  24.4 5.3 copy-start.40
  28.1 1.7 copy-start.28
  29.7 2.6 copy-start.63
  31.0 7.4 copy-start.38
  31.0 7.4 copy-start.64
  32.4 13.0 %copy-start.12 = (bf16[8,258,3,64]{1,0,3,2:T(8,128)(2,1)}, bf16[8,258,3,64]{1,0,3,2:T(8,128)(2,1)S(1)}, u32[]{:S(2)}) copy-start(bf16[8,258,3,64]{1,0,3,2:T(8,128)(2,1)S(1)} %reshape.271) | copy-start | bytes 2377732
  45.4 1.9 copy-start.14
  47.4 4.3 copy-start.2
  47.4 2.1 copy-start.18
  49.5 5.9 copy-start.37
  55.4 3.7 copy-start.19
  59.2 123.4 %copy-start.57 = (f32[768]{0:T(1024)S(1)}, f32[768]{0:T(1024)}, u32[]{:S(2)}) copy-start(f32[768]{0:T(1024)} %param.27) | copy-start | bytes 9220
  59.2 281.3 %all-reduce.10.cloned.1.call-start = ((), (), s32[]{:S(2)}) async-start(), calls=%async_computation.1 | async-start | bytes 12681216 | tf_op jit(solution)/shard_map/psum | solution.py:113
  188.4 2.7 copy-start.3
  189.4 2.2 copy-start.61
  189.4 2.2 copy-start.62
  191.5 2.7 copy-start.25
  191.5 3.0 copy-start.8
  194.6 18.7 %copy-start.23 = (f32[2064,768]{1,0:T(8,128)}, f32[2064,768]{1,0:T(8,128)S(1)}, u32[]{:S(2)}) copy-start(f32[2064,768]{1,0:T(8,128)S(1)} %convolution_add_fusion) | copy-start | bytes 19021828
  213.3 1.7 copy-start.65
  219.7 415.8 %all-reduce.14.cloned.1.call-start = ((), (), s32[]{:S(2)}) async-start(), calls=%async_computation.3 | async-start | bytes 25362432 | tf_op jit(solution)/shard_map/psum | solution.py:103
  225.2 1.6 copy-start.26
  347.0 6.8 copy-start.9
  353.8 2.7 copy-start.5
  356.5 1.7 copy-start.16
  375.5 10.9 %copy-start.15 = (bf16[8,258,3,64]{1,0,3,2:T(8,128)(2,1)S(1)}, bf16[8,258,3,64]{1,0,3,2:T(8,128)(2,1)}, u32[]{:S(2)}) copy-start(bf16[8,258,3,64]{1,0,3,2:T(8,128)(2,1)} %copy-done.14) | copy-start | bytes 2377732
  386.4 5.5 copy-start.4
  386.4 5.5 copy-start.13
  391.9 1.4 copy-start.24
  393.3 13.0 %copy-start.39 = (bf16[768,192]{0,1:T(8,128)(2,1)S(1)}, bf16[768,192]{0,1:T(8,128)(2,1)}, u32[]{:S(2)}) copy-start(bf16[768,192]{0,1:T(8,128)(2,1)} %param.21) | copy-start | bytes 884740
  397.1 11.3 %copy-start.21 = (bf16[2064,192]{0,1:T(8,128)(2,1)}, bf16[2064,192]{0,1:T(8,128)(2,1)S(1)}, u32[]{:S(2)}) copy-start(bf16[2064,192]{0,1:T(8,128)(2,1)S(1)} %convert_element_type.155) | copy-start | bytes 2377732
  404.2 3.2 copy-start.41
  412.2 468.1 %all-reduce.12.cloned.1.call-start = ((), (), s32[]{:S(2)}) async-start(), calls=%async_computation.2 | async-start | bytes 14155776 | tf_op jit(solution)/shard_map/psum | solution.py:170
  422.6 7.4 copy-start.10
  422.6 7.4 copy-start.27
  430.0 4.4 copy-start.17
  430.0 4.4 copy-start.20
  430.0 6.1 copy-start.6
  430.0 6.1 copy-start.22
  439.6 195.9 %copy-start.59 = (f32[768]{0:T(1024)S(1)}, f32[768]{0:T(1024)}, u32[]{:S(2)}) copy-start(f32[768]{0:T(1024)} %param.31) | copy-start | bytes 9220
  642.7 8.8 copy-start.36
  642.7 8.8 copy-start.44
  642.7 8.8 copy-start.46
  646.5 12.2 %slice-start = ((s8[6340608]{0:T(1024)(128)(4,1)}), s8[4194304]{0:T(1024)(128)(4,1)S(1)}, s32[]{:S(2)}) async-start(s8[6340608]{0:T(1024)(128)(4,1)} %bitcast.70), calls=%async_computation.4 | async-start | bytes 8388608
  651.5 7.1 copy-start.48
  651.5 7.2 slice-start.1
  658.7 7.8 copy-start.11
  679.1 7.7 copy-start.53
  679.1 7.7 copy-start.54
  679.1 7.7 copy-start.60
  880.3 7.9 copy-start.30
  880.3 9.3 %copy-start.29 = (f32[768,768]{1,0:T(8,128)S(1)}, f32[768,768]{1,0:T(8,128)}, u32[]{:S(2)}) copy-start(f32[768,768]{1,0:T(8,128)} %get-tuple-element.140) | copy-start | bytes 7077892
  880.3 10.7 %copy-start.1 = (bf16[768,768]{1,0:T(8,128)(2,1)S(1)}, bf16[768,768]{1,0:T(8,128)(2,1)}, u32[]{:S(2)}) copy-start(bf16[768,768]{1,0:T(8,128)(2,1)} %param.30) | copy-start | bytes 3538948
  (8 other events, 7.6 us)
Sparse Core Ops, SparseCore 0:
  59.3 123.2 all-reduce.7
  219.8 120.6 all-reduce.9
  412.3 223.0 all-reduce.13
  642.3 237.8 all-reduce.11
where the time goes:
time: 906 us; the launch traced here: 898 us
  waiting for transfers between devices  569 us (63%)
  matrix products  94.5 us (10%)
  local copies, waits for them, and re-layouts  92.1 us (10%)
  other arithmetic  86.8 us (10%)
  blocking collectives  39.8 us (4%)
  between operations  14.8 us (2%)
    psum x1, waiting for transfers between devices, shards(): branch_two = lax.psum(multiply(active_reduced, w_down), 'tensor') + b_down  192 us
    psum x1, waiting for transfers between devices, shards(): summed = lax.psum(mlp_group + attn_group, 'dp')  154 us
    psum x1, waiting for transfers between devices, shards(): branch = lax.psum(multiply(mixture, w_out), 'tensor') + b_out  115 us
    psum x1, waiting for transfers between devices, shards(): grad_normed_two = lax.psum(contract_cols(grad_hidden, w_up), 'tensor')  109 us
    psum x1, blocking collectives, shards(): summed = lax.psum(mlp_group + attn_group, 'dp')  39.8 us
    unnamed x145, local copies, waits for them, and re-layouts  37 us
    dot_general x6, matrix products, contract_cols(): lax.dot_general(left_mat, right_mat, (((1,), (1,)), ((), ())), preferred_...  30.3 us
    dot_general x6, matrix products, multiply(): return jnp.dot(left_mat, right_mat, preferred_element_type=jnp.float32)  20 us
  transfers between devices with their start and end apart: 4, of which 4 were waited for; matrix products, arithmetic and copies ran while one was open for 11% of the time, Pallas kernels for 0%

commit v1 on v0

--- a/solution.py
+++ b/solution.py
@@ -1,3 +1,4 @@
+import functools
 import math
 import jax
 import jax.numpy as jnp
@@ -6,6 +7,13 @@
 
 HEAD_DIM = 64
 NORM_EPSILON = 1e-05
+
+
+def forms_create(xin, peer_axis):
+    return jnp.sum(jax.lax.all_gather(xin, axis_name=peer_axis), axis=0)
+
+
+wait_waves = functools.partial(forms_create, peer_axis="tensor")
 
 
 def layer_norm(source_tokens, gain, shift):
@@ -93,7 +101,7 @@
         "shqk,skhc->sqhc", probs_low, head_values, preferred_element_type=jnp.float32
     )
     mixture = mixture.reshape(row_count, local_width).astype(jnp.bfloat16)
-    branch = lax.psum(multiply(mixture, w_out), "tensor") + b_out
+    branch = wait_waves(multiply(mixture, w_out)) + b_out
     middle = inputs + branch
     normed_two, norm_two_back = jax.vjp(layer_norm, middle, gain_two, shift_two)
     normed_two_low = normed_two.astype(jnp.bfloat16)

time: 906 us -> 969 us (1.070)
  waiting for transfers between devices: 569 us -> 609 us
  other arithmetic: 86.8 us -> 111 us
    all_gather x0 -> x1, waiting for transfers between devices: none -> 151 us  [forms_create(): return jnp.sum(jax.lax.all_gather(xin, axis_name=peer_axis), axis=0)]
    psum x1 -> x0, waiting for transfers between devices: 115 us -> none  [shards(): branch = lax.psum(multiply(mixture, w_out), 'tensor') + b_out]
    reduce_sum x0 -> x1, other arithmetic: none -> 12.5 us  [forms_create(): return jnp.sum(jax.lax.all_gather(xin, axis_name=peer_axis), axis=0)]
    unnamed x145 -> x141, local copies, waits for them, and re-layouts: 37 us -> 37.2 us
  transfers between devices with their start and end apart: 4 -> 4, of which waited for: 4 -> 4; matrix products, arithmetic and copies ran while one was open for 11% -> 10% of each run, Pallas kernels for 0% -> 0%
where the time goes in v1:
time: 969 us; the launch traced here: 960 us
  waiting for transfers between devices  609 us (63%)
  other arithmetic  111 us (11%)
  matrix products  94.6 us (10%)
  local copies, waits for them, and re-layouts  88.9 us (9%)
  blocking collectives  40.1 us (4%)
  between operations  15.1 us (2%)
    psum x1, waiting for transfers between devices, shards(): branch_two = lax.psum(multiply(active_reduced, w_down), 'tensor') + b_down  197 us
    psum x1, waiting for transfers between devices, shards(): summed = lax.psum(mlp_group + attn_group, 'dp')  153 us
    all_gather x1, waiting for transfers between devices, forms_create(): return jnp.sum(jax.lax.all_gather(xin, axis_name=peer_axis), axis=0)  151 us
    psum x1, waiting for transfers between devices, shards(): grad_normed_two = lax.psum(contract_cols(grad_hidden, w_up), 'tensor')  109 us
    psum x1, blocking collectives, shards(): summed = lax.psum(mlp_group + attn_group, 'dp')  40.1 us
    unnamed x141, local copies, waits for them, and re-layouts  37.2 us
    dot_general x6, matrix products, contract_cols(): lax.dot_general(left_mat, right_mat, (((1,), (1,)), ((), ())), preferred_...  29.7 us
    dot_general x6, matrix products, multiply(): return jnp.dot(left_mat, right_mat, preferred_element_type=jnp.float32)  19.8 us
  transfers between devices with their start and end apart: 4, of which 4 were waited for; matrix products, arithmetic and copies ran while one was open for 10% of the time, Pallas kernels for 0%

profile of v1, /device:TPU:0, one launch (start us, length us, event | category | flops | bytes accessed | tf_op | source)
XLA Modules:
  0.0 959.8 jit_solution(933450291314227638)
XLA Ops:
  8.2 3.1 multiply_reduce_fusion.8
  11.4 3.4 multiply_reduce_fusion.3
  14.9 5.2 copy_convert_fusion
  20.8 5.0 reshape.315
  25.9 3.7 add_convert_fusion.4
  33.9 3.6 fusion.8
  37.5 2.4 reshape.308
  39.9 4.0 fusion.9
  43.9 3.0 reshape.309
  47.0 1.9 multiply_reduce_fusion.1
  48.9 1.8 exponential_reduce_fusion
  51.0 2.1 fusion.11
  53.1 1.7 copy.57
  54.9 2.1 convert_element_type.140
  57.0 3.6 fusion.34
  60.7 4.2 copy.58
  64.9 3.7 reshape.312
  68.5 150.8 %all-gather.3.cloned.1.call-done = f32[8256,768]{1,0:T(8,128)} async-done(((f32[2064,768]{1,0:T(8,128)}), f32[8256,768]{1,0:T(8,128)}) %all-gather.3.cloned.1.call-update) | async-done | bytes 25362448 | tf_op jit(solution)/shard_map/all_gather | solution.py:13
  219.3 12.5 %reduce_sum.190 = f32[2064,768]{1,0:T(8,128)} reduce(f32[4,2064,768]{2,1,0:T(8,128)} %bitcast.73, f32[]{:T(128)} %constant.39.clone.1), dimensions={0}, to_apply=%region_4.5 | reduce | flops 4755456 | bytes 31703044 | tf_op jit(solution)/shard_map/reduce_sum | solution.py:13
  231.8 5.0 reduce_sum.191
  236.9 7.8 add_convert_fusion
  245.6 2.7 multiply_reduce_fusion.2
  248.5 7.3 add_convert_fusion.3
  255.8 2.7 convolution_add_fusion
  258.9 18.1 %convert_reduce_fusion.1 = (f32[768]{0:T(1024)S(1)}, bf16[2064,768]{1,0:T(8,128)(2,1)S(1)}, f32[2064,768]{1,0:T(8,128)}) fusion(f32[2064,768]{1,0:T(8,128)S(1)} %convolution_add_fusion, bf16[2064,768]{1,0:T(8,128)(2,1)S(1)} %copy-done.8, bf16[768,768]{1,0:T(8,128)(2,1)S(1)} %copy-done), kind=kOutput, calls=%fused_computation.16 | convolution fusion | flops 2552093952 | bytes 20204544 | tf_op jit(solution)/shard_map/dot_general | solution.py:41
  278.6 4.6 fusion.36
  283.7 5.5 multiply_convert_fusion.1
  290.9 4.6 fusion.35
  295.4 108.5 %all-reduce.7.cloned.1.call-done = f32[2064,768]{1,0:T(8,128)} async-done(((f32[2064,768]{1,0:T(8,128)}), f32[2064,768]{1,0:T(8,128)}) %all-reduce.7.cloned.1.call-update) | async-done | bytes 6340624 | tf_op jit(solution)/shard_map/psum | solution.py:121
  404.0 5.9 multiply_reduce_fusion.4
  409.9 6.8 fusion.33
  423.6 6.8 convert_reduce_fusion.3
  430.4 7.6 multiply_reduce_fusion
  438.1 10.9 %multiply_convert_fusion = bf16[8,3,258,258]{2,3,1,0:T(8,128)(2,1)} fusion(f32[8,3,258,258]{2,3,1,0:T(8,128)} %get-tuple-element.92, f32[8,3,258,258]{2,3,1,0:T(8,128)} %copy-done.2, f32[8,3,258]{2,1,0:T(4,128)S(1)} %get-tuple-element.91, f32[8,3,258]{2,1,0:T(4,128)S(1)} %log_add_fusion), kind=kLoop, calls=%fused_computation | loop fusion | flops 7987680 | bytes 16024896 | tf_op jit(solution)/shard_map/convert_element_type | solution.py:143
  449.0 5.5 fusion.14
  457.6 2.1 convert_element_type.157
  459.7 3.3 copy.66
  463.0 2.1 convert_element_type.154
  465.0 1.7 copy.63
  466.7 2.1 convert_element_type.151
  471.0 3.7 add_add_fusion.3
  474.8 3.7 convert_element_type.159
  478.5 8.5 fusion.40
  487.1 4.4 fusion.41
  491.5 1.7 fusion.39
  493.2 1.7 fusion.44
  494.9 1.7 fusion.43
  496.7 1.7 fusion.42
  498.4 2.4 convert_reduce_fusion
  501.0 197.0 %all-reduce.11.cloned.1.call-done = (f32[2064,768]{1,0:T(8,128)}, f32[2064,768]{1,0:T(8,128)}) async-done(((f32[2064,768]{1,0:T(8,128)}, f32[2064,768]{1,0:T(8,128)}), (f32[2064,768]{1,0:T(8,128)}, f32[2064,768]{1,0:T(8,128)})) %all-reduce.11.cloned.1.call-update) | async-done | bytes 12681232 | tf_op jit(solution)/shard_map/psum | solution.py:111
  698.0 7.2 add_convert_fusion.2
  705.2 3.8 reshape.311
  709.1 4.9 copy.70
  714.0 7.1 multiply_reduce_fusion.5
  721.2 7.7 fusion.32
  728.9 7.4 add_multiply_fusion
  736.3 5.0 reshape.314
  741.3 7.8 copy.71
  749.2 40.1 %all-reduce = (f32[192]{0:T(256)}, f32[192]{0:T(256)}, f32[768]{0:T(1024)}, f32[768]{0:T(1024)}, f32[768]{0:T(1024)}, /*index=5*/f32[768]{0:T(1024)}, f32[768]{0:T(1024)}, f32[768]{0:T(1024)}, f32[768]{0:T(1024)}) all-reduce(f32[192]{0:T(256)S(1)} %reduce_sum.231, ...), channel_id=1, replica_groups=mesh['dp'=8,'tensor'=4] {'dp'}, use_global_device_ids=true, to_apply=%region_20.21 | all-reduce | flops 5760 | bytes 46080 | tf_op jit(solution)/shard_map/psum | solution.py:178
  789.3 152.8 %all-reduce.9.cloned.1.call-done = (f32[768,192]{0,1:T(8,128)}, f32[768,192]{0,1:T(8,128)}, f32[768,192]{0,1:T(8,128)}, f32[192,768]{1,0:T(8,128)}, f32[768,768]{1,0:T(8,128)}, /*index=5*/f32[768,768]{1,0:T(8,128)}) async-done(((f32[768,192]{0,1:T(8,128)}, f32[768,192]{0,1:T(8,128)}, f32[768,192]{0,1:T(8,128)}, f32[192,768]{1,0:T(8,128)}, f32[768,768]{1,0:T(8,128)}, /*index=5*/f32[768,768]{1,0:T(8,128)}), ...) | async-done | bytes 7077904 | tf_op jit(solution)/shard_map/psum | solution.py:178
  942.1 2.1 copy.119
  944.2 2.0 copy.120
  946.2 1.9 copy.121
  948.1 1.9 copy.122
  (173 shorter events, 27.0 us)
Async XLA Ops:
  7.2 251.4 %copy-start = (bf16[768,768]{1,0:T(8,128)(2,1)S(1)}, bf16[768,768]{1,0:T(8,128)(2,1)}, u32[]{:S(2)}) copy-start(bf16[768,768]{1,0:T(8,128)(2,1)} %param.30) | copy-start | bytes 3538948
  7.2 212.1 %all-gather.3.cloned.1.call-start = ((), (), s32[]{:S(2)}) async-start(), calls=%async_computation.1 | async-start | bytes 31703040 | tf_op jit(solution)/shard_map/all_gather | solution.py:13
  8.1 12.0 %copy-start.33 = (f32[8,258]{1,0:T(8,128)}, f32[8,258]{1,0:T(8,128)S(1)}, u32[]{:S(2)}) copy-start(f32[8,258]{1,0:T(8,128)S(1)} %broadcast_select_fusion) | copy-start | bytes 24772
  8.2 240.3 %copy-start.31 = (f32[2064]{0:T(1024)}, f32[2064]{0:T(1024)S(1)}, u32[]{:S(2)}) copy-start(f32[2064]{0:T(1024)S(1)} %select_n.13) | copy-start | bytes 24772
  11.3 8.8 copy-start.46
  11.4 14.4 %copy-start.42 = (f32[2064]{0:T(1024)}, f32[2064]{0:T(1024)S(1)}, u32[]{:S(2)}) copy-start(f32[2064]{0:T(1024)S(1)} %div.41) | copy-start | bytes 24772
  20.8 5.1 copy-start.48
  20.8 5.0 copy-start.44
  20.8 5.0 copy-start.50
  20.8 5.0 copy-start.55
  25.9 5.4 copy-start.39
  31.2 2.6 copy-start.61
  32.5 7.4 copy-start.37
  32.5 7.4 copy-start.62
  33.9 13.0 %copy-start.12 = (bf16[8,258,3,64]{1,0,3,2:T(8,128)(2,1)}, bf16[8,258,3,64]{1,0,3,2:T(8,128)(2,1)S(1)}, u32[]{:S(2)}) copy-start(bf16[8,258,3,64]{1,0,3,2:T(8,128)(2,1)S(1)} %reshape.310) | copy-start | bytes 2377732
  46.9 1.9 copy-start.14
  48.9 4.3 copy-start.2
  48.9 2.1 copy-start.18
  51.0 5.9 copy-start.35
  56.9 3.7 copy-start.19
  60.6 343.4 %all-reduce.7.cloned.1.call-start = ((), (), s32[]{:S(2)}) async-start(), calls=%async_computation | async-start | bytes 12681216 | tf_op jit(solution)/shard_map/psum | solution.py:121
  231.8 5.0 copy-start.34
  231.8 5.0 copy-start.47
  231.8 5.0 copy-start.52
  231.8 5.0 copy-start.53
  231.8 5.0 copy-start.56
  236.9 7.8 copy-start.3
  236.9 8.7 copy-start.5
  244.6 3.8 copy-start.54
  244.6 3.8 copy-start.57
  248.5 7.4 copy-start.59
  248.5 7.3 copy-start.60
  255.8 2.7 copy-start.28
  255.8 3.0 copy-start.8
  258.9 18.1 %copy-start.23 = (f32[2064,768]{1,0:T(8,128)}, f32[2064,768]{1,0:T(8,128)S(1)}, u32[]{:S(2)}) copy-start(f32[2064,768]{1,0:T(8,128)S(1)} %convolution_add_fusion) | copy-start | bytes 19021828
  283.3 414.7 %all-reduce.11.cloned.1.call-start = ((), (), s32[]{:S(2)}) async-start(), calls=%async_computation.3 | async-start | bytes 25362432 | tf_op jit(solution)/shard_map/psum | solution.py:111
  409.9 6.8 copy-start.9
  416.7 2.6 copy-start.6
  416.7 4.3 copy-start.36
  438.0 10.9 %copy-start.15 = (bf16[8,258,3,64]{1,0,3,2:T(8,128)(2,1)S(1)}, bf16[8,258,3,64]{1,0,3,2:T(8,128)(2,1)}, u32[]{:S(2)}) copy-start(bf16[8,258,3,64]{1,0,3,2:T(8,128)(2,1)} %copy-done.14) | copy-start | bytes 2377732
  449.0 5.5 copy-start.4
  449.0 5.5 copy-start.13
  455.9 13.0 %copy-start.38 = (bf16[768,192]{0,1:T(8,128)(2,1)S(1)}, bf16[768,192]{0,1:T(8,128)(2,1)}, u32[]{:S(2)}) copy-start(bf16[768,192]{0,1:T(8,128)(2,1)} %param.21) | copy-start | bytes 884740
  459.7 11.3 %copy-start.21 = (bf16[2064,192]{0,1:T(8,128)(2,1)}, bf16[2064,192]{0,1:T(8,128)(2,1)S(1)}, u32[]{:S(2)}) copy-start(bf16[2064,192]{0,1:T(8,128)(2,1)S(1)} %convert_element_type.157) | copy-start | bytes 2377732
  466.7 3.2 copy-start.40
  474.8 467.3 %all-reduce.9.cloned.1.call-start = ((), (), s32[]{:S(2)}) async-start(), calls=%async_computation.2 | async-start | bytes 14155776 | tf_op jit(solution)/shard_map/psum | solution.py:178
  478.5 8.5 copy-start.10
  478.5 8.5 copy-start.26
  487.1 4.4 copy-start.17
  487.1 4.4 copy-start.20
  487.1 6.1 copy-start.7
  487.1 6.1 copy-start.22
  496.7 201.3 %copy-start.58 = (f32[768]{0:T(1024)S(1)}, f32[768]{0:T(1024)}, u32[]{:S(2)}) copy-start(f32[768]{0:T(1024)} %param.31) | copy-start | bytes 9220
  705.2 8.7 copy-start.32
  705.2 8.7 copy-start.43
  705.2 8.7 copy-start.45
  705.2 8.7 copy-start.51
  709.1 12.1 %slice-start = ((s8[6340608]{0:T(1024)(128)(4,1)}), s8[4194304]{0:T(1024)(128)(4,1)S(1)}, s32[]{:S(2)}) async-start(s8[6340608]{0:T(1024)(128)(4,1)} %bitcast.71), calls=%async_computation.4 | async-start | bytes 8388608
  714.0 7.2 copy-start.49
  714.0 7.2 slice-start.1
  721.2 7.7 copy-start.11
  942.1 7.9 copy-start.30
  942.1 9.3 copy-start.29
  942.1 10.7 %copy-start.1 = (bf16[768,768]{1,0:T(8,128)(2,1)S(1)}, bf16[768,768]{1,0:T(8,128)(2,1)}, u32[]{:S(2)}) copy-start(bf16[768,768]{1,0:T(8,128)(2,1)} %param.30) | copy-start | bytes 3538948
  (6 other events, 9.2 us)
Sparse Core Ops, SparseCore 0:
  60.7 158.5 all-gather.2
  283.4 120.5 all-reduce.6
  474.9 223.0 all-reduce.10
  704.1 237.9 all-reduce.8
